TPU v7x, 32 devices: a whole 2x2x4 slice. The times are simulated.
32 devices in a mesh: gx: 8 (over z, x), gy: 4 (over y, core).
Axes of the slice: x: 2, y: 2, z: 4, core: 2. Of those that a mesh axis runs over, the one named last changes fastest.
Arguments:
- orbitals: bfloat16 [20000, 200], P('gx'), may hold values from -6 to 6
- projector: bfloat16 [6016, 20000], P('gy', 'gx'), may hold values from -0.0390625 to 0.0390625
- integrals: bfloat16 [8, 6016, 6016], P('gx', 'gy'), may hold values from -1 to 1
Outputs:
- exchange_matrix: float32 [6016, 6016], P('gx', 'gy')
- exchange_orbitals: float32 [20000, 200], P('gx', 'gy')
- energy_mean: float32 [], replicated
- trace_mean: float32 [], replicated
All inputs are finite; a program needn't handle non-finite values.
Results may differ from a plain program's by a relative error of at most 0.008.
Values may be sent and summed in bfloat16 or wider, within the bound.
No kernel may reach another device: no remote copies, remote signals or barrier semaphores. Data moves between devices by JAX's collectives and lax.ppermute only.
A program may use at most 128 MiB of HBM per device.

v0:
```python
import jax
import jax.numpy as jnp
from jax import lax
from jax.sharding import PartitionSpec as P


def spread(block, axis, holder):
    block = jnp.where(lax.axis_index(axis) == holder, block, jnp.zeros_like(block))
    return lax.psum(block, axis)


def on_device(orbitals, projector, integrals):
    part_rows = projector.shape[0]
    partial_value = jnp.dot(projector, orbitals, preferred_element_type=jnp.float32)
    own_admm = lax.psum(partial_value, "gx").astype(jnp.bfloat16)
    admm = lax.all_gather(own_admm, "gy", axis=0, tiled=True)
    half = lax.dot_general(
        integrals, admm, (((2,), (0,)), ((), ())), preferred_element_type=jnp.float32
    ).astype(jnp.bfloat16)
    size_x = lax.axis_size("gx")
    block_rows = admm.shape[0] // size_x
    index_x = lax.axis_index("gx")
    index_y = lax.axis_index("gy")
    all_half = lax.all_gather(half, "gx", axis=0, tiled=True)
    first_row = index_x * block_rows
    root = first_row // part_rows
    offset = jnp.clip(first_row - index_y * part_rows, 0, part_rows - block_rows)
    mine = lax.dynamic_slice_in_dim(all_half, offset, block_rows, 1)
    columns = spread(mine, "gy", root)
    exchange = lax.dot_general(
        columns, all_half, (((0, 2), (0, 2)), ((), ())), preferred_element_type=jnp.float32
    )
    row_ids = index_x * block_rows + lax.iota(jnp.int32, block_rows)
    col_ids = index_y * part_rows + lax.iota(jnp.int32, part_rows)
    diag_mask = row_ids[:, None] == col_ids[None, :]
    trace_part = jnp.sum(jnp.where(diag_mask, exchange, 0.0))
    trace_total = lax.psum(trace_part, ("gx", "gy"))
    admm_wide = admm.astype(jnp.float32)
    col_orbs = lax.dynamic_slice_in_dim(admm_wide, index_x * block_rows, block_rows, 0)
    row_orbs = lax.dynamic_slice_in_dim(admm_wide, index_y * part_rows, part_rows, 0)
    applied_part = lax.dot_general(
        exchange,
        col_orbs,
        (((0,), (0,)), ((), ())),
        precision=lax.Precision.HIGHEST,
        preferred_element_type=jnp.float32,
    )
    energy_part = jnp.sum(row_orbs * applied_part)
    energy_total = lax.psum(energy_part, ("gx", "gy"))
    applied = lax.psum(applied_part, "gx")
    applied_low = applied.astype(jnp.bfloat16)
    back_part = lax.dot_general(
        projector, applied_low, (((0,), (0,)), ((), ())), preferred_element_type=jnp.float32
    )
    back = lax.psum_scatter(back_part, "gy", scatter_dimension=1, tiled=True)
    total_adm = admm.shape[0]
    energy_mean = -0.5 * energy_total / (total_adm * admm.shape[1])
    trace_mean = trace_total / total_adm
    return (exchange, back, energy_mean, trace_mean)


def solution(mesh):
    return jax.shard_map(
        on_device,
        mesh=mesh,
        in_specs=(P("gx", None), P("gy", "gx"), P("gx", "gy", None)),
        out_specs=(P("gx", "gy"), P("gx", "gy"), P(), P()),
        check_vma=False,
    )
```

profile of v0, /device:TPU:12, one launch (start us, length us, event | category | flops | bytes accessed | tf_op | source)
XLA Modules:
  0.0 447.2 jit_solution(2069144303628339878)
XLA Ops:
  7.2 0.0 copy-start
  7.2 0.0 all-gather.6.cloned.1.call-start
  7.2 1.2 copy-done
  8.4 4.9 %fusion.13 = f32[1504,200]{0,1:T(8,128)S(1)} fusion(bf16[1504,2500]{0,1:T(8,128)(2,1)} %param.4, bf16[2500,200]{0,1:T(8,128)(2,1)S(1)} %copy-done), kind=kOutput, calls=%fused_computation.17 | convolution fusion | flops 1504000000 | bytes 9723200 | tf_op jit(solution)/shard_map/dot_general | solution.py:14
  13.3 72.9 %all-reduce.8 = bf16[1504,200]{0,1:T(8,128)(2,1)} all-reduce(f32[1504,200]{0,1:T(8,128)S(1)} %fusion.13), channel_id=1, replica_groups=mesh['gx'=8,'gy'=4] {'gx'}, use_global_device_ids=true, to_apply=%region_0.0 | all-reduce | flops 300800 | bytes 1804800 | tf_op jit(solution)/shard_map/psum | solution.py:15
  86.2 0.0 all-gather.6.cloned.1.call-update
  86.2 0.0 all-gather.8.cloned.1.call-start
  86.3 23.8 %all-gather.6.cloned.1.call-done = bf16[4,1504,200]{1,2,0:T(8,128)(2,1)} async-done(((bf16[1,1504,200]{1,2,0:T(8,128)(2,1)}), bf16[4,1504,200]{1,2,0:T(8,128)(2,1)}) %all-gather.6.cloned.1.call-update) | async-done | bytes 2406416 | tf_op jit(solution)/shard_map/all_gather | solution.py:16
  110.1 3.0 copy.8
  113.1 4.4 reshape.24
  117.5 13.3 %fusion.6 = bf16[1,1504,200]{1,2,0:T(8,128)(2,1)} fusion(bf16[6016,200]{0,1:T(8,128)(2,1)} %reshape.24, bf16[1,1504,6016]{2,1,0:T(8,128)(2,1)} %param.5), kind=kOutput, calls=%fused_computation.7 | convolution fusion | flops 3619526400 | bytes 21104128 | tf_op jit(solution)/shard_map/dot_general | solution.py:17
  130.8 0.0 all-gather.8.cloned.1.call-update
  130.8 0.2 all-reduce.7.cloned.1.call-start
  131.1 81.9 %all-gather.8.cloned.1.call-done = bf16[8,1504,200]{1,2,0:T(8,128)(2,1)} async-done(((bf16[1,1504,200]{1,2,0:T(8,128)(2,1)}), bf16[8,1504,200]{1,2,0:T(8,128)(2,1)}) %all-gather.8.cloned.1.call-update) | async-done | bytes 4812816 | tf_op jit(solution)/shard_map/all_gather | solution.py:24
  213.0 4.8 %dynamic-slice_select_fusion = bf16[8,752,200]{1,2,0:T(8,128)(2,1)} fusion(bf16[8,1504,200]{1,2,0:T(8,128)(2,1)} %all-gather.8.cloned.1.call-done, s32[]{:T(128)S(6)} %min.4, pred[]{:T(512)S(6)} %eq.16), kind=kLoop, calls=%fused_computation.6 | loop fusion | flops 1203200 | bytes 4812805 | tf_op jit(solution)/shard_map/jit(_where)/select_n | solution.py:8
  217.8 0.0 all-reduce.7.cloned.1.call-update
  217.9 55.5 %all-reduce.7.cloned.1.call-done = bf16[8,752,200]{1,2,0:T(8,128)(2,1)} async-done(((bf16[8,752,200]{1,2,0:T(8,128)(2,1)}), bf16[8,752,200]{1,2,0:T(8,128)(2,1)}) %all-reduce.7.cloned.1.call-update) | async-done | bytes 2406416 | tf_op jit(solution)/shard_map/psum | solution.py:9
  273.4 8.1 %select_reduce_fusion = (f32[]{:T(128)}, f32[752,1504]{1,0:T(8,128)S(1)}) fusion(s32[1504]{0:T(1024)S(1)} %iota_add_fusion, s32[752]{0:T(1024)S(1)} %iota_add_fusion.1, bf16[8,752,200]{1,2,0:T(8,128)(2,1)} %all-reduce.7.cloned.1.call-done, bf16[8,1504,200]{1,2,0:T(8,128)(2,1)} %all-gather.8.cloned.1.call-done), kind=kOutput, calls=%fused_computation.2 | convolution fusion | flops 3622618624 | bytes 11752260 | tf_op jit(solution)/shard_map/dot_general | solution.py:30
  281.5 0.0 copy-start.1
  281.5 5.0 %multiply_reduce_fusion = (f32[]{:T(128)}, f32[1504,200]{0,1:T(8,128)S(1)}) fusion(bf16[6016,200]{0,1:T(8,128)(2,1)} %reshape.24, s32[]{:T(128)S(6)} %select_n.28, f32[752,1504]{1,0:T(8,128)S(1)} %get-tuple-element.9, s32[]{:T(128)S(6)} %select_n.27), kind=kOutput, calls=%fused_computation.8 | convolution fusion | flops 2715321600 | bytes 6648844 | tf_op jit(solution)/shard_map/dot_general | solution.py:41
  286.6 0.0 copy-done.1
  286.6 72.6 %all-reduce.9 = bf16[1504,200]{0,1:T(8,128)(2,1)S(1)} all-reduce(f32[1504,200]{0,1:T(8,128)S(1)} %get-tuple-element.7), channel_id=1, replica_groups=mesh['gx'=8,'gy'=4] {'gx'}, use_global_device_ids=true, to_apply=%region_2.3 | all-reduce | flops 300800 | bytes 1804800 | tf_op jit(solution)/shard_map/psum | solution.py:50
  359.2 7.0 %convolution_bitcast_fusion = f32[2500,200]{0,1:T(8,128)} fusion(bf16[1504,2500]{0,1:T(8,128)(2,1)} %param.4, bf16[1504,200]{0,1:T(8,128)(2,1)S(1)} %all-reduce.9), kind=kOutput, calls=%fused_computation.3 | convolution fusion | flops 1504000000 | bytes 10121600 | tf_op jit(solution)/shard_map/dot_general | solution.py:52
  366.1 0.0 copy-start.2
  366.1 24.2 %fusion = f32[2500,56]{0,1:T(8,128)S(1)} fusion(f32[2500,200]{0,1:T(8,128)} %convolution_bitcast_fusion), kind=kCustom, calls=%all-reduce-scatter | all-reduce-scatter fusion | flops 560001 | bytes 2560512
  390.3 1.9 collective-permute-start
  392.2 0.0 copy-done.2
  392.3 0.6 dynamic-slice.5
  393.5 42.3 %all-reduce.2 = (f32[]{:T(128)}, f32[]{:T(128)}) all-reduce(f32[]{:T(128)} %get-tuple-element.6, f32[]{:T(128)} %get-tuple-element.8), channel_id=1, replica_groups=mesh['gx'=8,'gy'=4] {'gx','gy'}, use_global_device_ids=true, to_apply=%region_5.6 | all-reduce | flops 2 | bytes 16 | tf_op jit(solution)/shard_map/psum | solution.py:49
  437.1 0.0 collective-permute-done
  437.1 0.4 concatenate
  437.6 0.9 constant_dynamic-slice_fusion
  (3 shorter events, 0.0 us)
Async XLA Ops:
  7.2 1.2 copy-start
  7.2 102.9 %all-gather.6.cloned.1.call-start = ((), (), s32[]{:S(2)}) async-start(), calls=%async_computation.1 | async-start | bytes 3072000 | tf_op jit(solution)/shard_map/all_gather | solution.py:16
  86.2 126.8 %all-gather.8.cloned.1.call-start = ((), (), s32[]{:S(2)}) async-start(), calls=%async_computation.2 | async-start | bytes 5529600 | tf_op jit(solution)/shard_map/all_gather | solution.py:24
  130.8 142.6 %all-reduce.7.cloned.1.call-start = ((), (), s32[]{:S(2)}) async-start(), calls=%async_computation | async-start | bytes 4915200 | tf_op jit(solution)/shard_map/psum | solution.py:9
  281.5 5.0 %copy-start.1 = (f32[752,1504]{1,0:T(8,128)}, f32[752,1504]{1,0:T(8,128)S(1)}, u32[]{:S(2)}) copy-start(f32[752,1504]{1,0:T(8,128)S(1)} %get-tuple-element.9) | copy-start | bytes 13572100
  366.1 26.1 %copy-start.2 = (u32[32]{0:T(128)S(1)}, u32[32]{0:T(128)}, u32[]{:S(2)}) copy-start(u32[32]{0:T(128)} %constant.44) | copy-start | bytes 388
  390.3 46.8 %collective-permute-start = (f32[2500,18]{0,1:T(8,128)S(1)}, f32[2500,18]{0,1:T(8,128)S(1)}, u32[]{:S(2)}, u32[]{:S(2)}) collective-permute-start(f32[2500,18]{0,1:T(8,128)S(1)} %slice), channel_id=1, source_target_pairs={{0,1},{1,2},{2,3},{4,5},{5,6},{6,7},{8,9},{9,10},{10,11},{12,13},{... | collective-permute-start | bytes 540008
Sparse Core Ops, SparseCore 0:
  86.3 23.7 all-gather.5
  130.9 82.0 all-gather.7
  218.0 55.3 all-reduce.6
where the time goes:
time: 448 us; the launch traced here: 447 us
  blocking collectives  212 us (47%)
  waiting for transfers between devices  161 us (36%)
  matrix products  38.4 us (9%)
  between operations  18.1 us (4%)
  local copies, waits for them, and re-layouts  10.4 us (2%)
  other arithmetic  4.83 us (1%)
    all_gather x1, waiting for transfers between devices, on_device(): all_half = lax.all_gather(half, 'gx', axis=0, tiled=True)  81.9 us
    psum x1, blocking collectives, on_device(): own_admm = lax.psum(partial_value, 'gx').astype(jnp.bfloat16)  72.9 us
    psum x1, blocking collectives, on_device(): applied = lax.psum(applied_part, 'gx')  72.6 us
    psum x1, waiting for transfers between devices, spread(): return lax.psum(block, axis)  55.5 us
    psum x1, blocking collectives, on_device(): energy_total = lax.psum(energy_part, ('gx', 'gy'))  42.3 us
    unnamed x1, blocking collectives  24.2 us
    all_gather x1, waiting for transfers between devices, on_device(): admm = lax.all_gather(own_admm, 'gy', axis=0, tiled=True)  23.8 us
    dot_general x1, matrix products, on_device(): lax.dot_general(integrals, admm, (((2,), (0,)), ((), ())), preferred_elem...  13.3 us
  transfers between devices with their start and end apart: 4, of which 3 were waited for; matrix products, arithmetic and copies ran while one was open for 0% of the time, Pallas kernels for 0%

commit v1 on v0

--- a/solution.py
+++ b/solution.py
@@ -6,7 +6,7 @@
 
 def spread(block, axis, holder):
     block = jnp.where(lax.axis_index(axis) == holder, block, jnp.zeros_like(block))
-    return lax.psum(block, axis)
+    return jnp.sum(lax.all_gather(block, axis), axis=0)
 
 
 def on_device(orbitals, projector, integrals):

time: 448 us -> 462 us (1.031)
  waiting for transfers between devices: 161 us -> 170 us
  other arithmetic: 4.83 us -> 11.2 us
    all_gather x0 -> x1, waiting for transfers between devices: none -> 64.6 us  [spread(): return jnp.sum(lax.all_gather(block, axis), axis=0)]
    psum x1 -> x0, waiting for transfers between devices: 55.5 us -> none  [spread(): return lax.psum(block, axis)]
    reduce_sum x0 -> x1, other arithmetic: none -> 6.33 us  [spread(): return jnp.sum(lax.all_gather(block, axis), axis=0)]
where the time goes in v1:
time: 462 us; the launch traced here: 461 us
  blocking collectives  212 us (46%)
  waiting for transfers between devices  170 us (37%)
  matrix products  37.8 us (8%)
  between operations  18.1 us (4%)
  other arithmetic  11.2 us (2%)
  local copies, waits for them, and re-layouts  10.4 us (2%)
    all_gather x1, waiting for transfers between devices, on_device(): all_half = lax.all_gather(half, 'gx', axis=0, tiled=True)  81.9 us
    psum x1, blocking collectives, on_device(): own_admm = lax.psum(partial_value, 'gx').astype(jnp.bfloat16)  73.5 us
    psum x1, blocking collectives, on_device(): applied = lax.psum(applied_part, 'gx')  71.8 us
    all_gather x1, waiting for transfers between devices, spread(): return jnp.sum(lax.all_gather(block, axis), axis=0)  64.6 us
    psum x1, blocking collectives, on_device(): energy_total = lax.psum(energy_part, ('gx', 'gy'))  41.9 us
    unnamed x1, blocking collectives  24.7 us
    all_gather x1, waiting for transfers between devices, on_device(): admm = lax.all_gather(own_admm, 'gy', axis=0, tiled=True)  23.3 us
    dot_general x1, matrix products, on_device(): lax.dot_general(integrals, admm, (((2,), (0,)), ((), ())), preferred_elem...  13.3 us
  transfers between devices with their start and end apart: 4, of which 3 were waited for; matrix products, arithmetic and copies ran while one was open for 0% of the time, Pallas kernels for 0%

profile of v1, /device:TPU:12, one launch (start us, length us, event | category | flops | bytes accessed | tf_op | source)
XLA Modules:
  0.0 461.4 jit_solution(10496881365613317889)
XLA Ops:
  7.2 0.0 copy-start
  7.2 0.0 all-gather.10.cloned.1.call-start
  7.2 1.2 copy-done
  8.4 4.9 %fusion.13 = f32[1504,200]{0,1:T(8,128)S(1)} fusion(bf16[1504,2500]{0,1:T(8,128)(2,1)} %param.4, bf16[2500,200]{0,1:T(8,128)(2,1)S(1)} %copy-done), kind=kOutput, calls=%fused_computation.17 | convolution fusion | flops 1504000000 | bytes 9723200 | tf_op jit(solution)/shard_map/dot_general | solution.py:14
  13.3 73.5 %all-reduce.5 = bf16[1504,200]{0,1:T(8,128)(2,1)} all-reduce(f32[1504,200]{0,1:T(8,128)S(1)} %fusion.13), channel_id=1, replica_groups=mesh['gx'=8,'gy'=4] {'gx'}, use_global_device_ids=true, to_apply=%region_0.0 | all-reduce | flops 300800 | bytes 1804800 | tf_op jit(solution)/shard_map/psum | solution.py:15
  86.8 0.0 all-gather.10.cloned.1.call-update
  86.8 0.0 all-gather.12.cloned.1.call-start
  86.8 23.3 %all-gather.10.cloned.1.call-done = bf16[4,1504,200]{1,2,0:T(8,128)(2,1)} async-done(((bf16[1,1504,200]{1,2,0:T(8,128)(2,1)}), bf16[4,1504,200]{1,2,0:T(8,128)(2,1)}) %all-gather.10.cloned.1.call-update) | async-done | bytes 2406416 | tf_op jit(solution)/shard_map/all_gather | solution.py:16
  110.1 3.0 copy.8
  113.1 4.3 reshape.25
  117.4 13.3 %fusion.6 = bf16[1,1504,200]{1,2,0:T(8,128)(2,1)} fusion(bf16[6016,200]{0,1:T(8,128)(2,1)} %reshape.25, bf16[1,1504,6016]{2,1,0:T(8,128)(2,1)} %param.5), kind=kOutput, calls=%fused_computation.7 | convolution fusion | flops 3619526400 | bytes 21104128 | tf_op jit(solution)/shard_map/dot_general | solution.py:17
  130.7 0.0 all-gather.12.cloned.1.call-update
  130.8 0.2 all-gather.8.cloned.1.call-start
  131.0 81.9 %all-gather.12.cloned.1.call-done = bf16[8,1504,200]{1,2,0:T(8,128)(2,1)} async-done(((bf16[1,1504,200]{1,2,0:T(8,128)(2,1)}), bf16[8,1504,200]{1,2,0:T(8,128)(2,1)}) %all-gather.12.cloned.1.call-update) | async-done | bytes 4812816 | tf_op jit(solution)/shard_map/all_gather | solution.py:24
  212.9 4.8 %dynamic-slice_select_fusion = bf16[8,752,200]{1,2,0:T(8,128)(2,1)} fusion(bf16[8,1504,200]{1,2,0:T(8,128)(2,1)} %all-gather.12.cloned.1.call-done, s32[]{:T(128)S(6)} %min.4, pred[]{:T(512)S(6)} %eq.16), kind=kLoop, calls=%fused_computation.6 | loop fusion | flops 1203200 | bytes 4812805 | tf_op jit(solution)/shard_map/jit(_where)/select_n | solution.py:8
  217.8 0.0 all-gather.8.cloned.1.call-update
  217.8 64.6 %all-gather.8.cloned.1.call-done = bf16[32,752,200]{1,2,0:T(8,128)(2,1)} async-done(((bf16[8,752,200]{1,2,0:T(8,128)(2,1)}), bf16[32,752,200]{1,2,0:T(8,128)(2,1)}) %all-gather.8.cloned.1.call-update) | async-done | bytes 9625616 | tf_op jit(solution)/shard_map/all_gather | solution.py:9
  282.4 6.3 %reduce_sum.30 = bf16[8,752,200]{1,2,0:T(8,128)(2,1)S(1)} reduce(bf16[4,8,752,200]{2,3,1,0:T(8,128)(2,1)} %bitcast.32, bf16[]{:T(256)} %constant.34.clone.1), dimensions={0}, to_apply=%region_1.2 | reduce | flops 3609600 | bytes 12032002 | tf_op jit(solution)/shard_map/reduce_sum | solution.py:9
  288.8 7.5 %select_reduce_fusion = (f32[]{:T(128)}, f32[752,1504]{1,0:T(8,128)S(1)}) fusion(s32[1504]{0:T(1024)S(1)} %iota_add_fusion, s32[752]{0:T(1024)S(1)} %iota_add_fusion.1, bf16[8,752,200]{1,2,0:T(8,128)(2,1)S(1)} %reduce_sum.30, bf16[8,1504,200]{1,2,0:T(8,128)(2,1)} %all-gather.12.cloned.1.call-done), kind=kOutput, calls=%fused_computation.2 | convolution fusion | flops 3622618624 | bytes 11752260 | tf_op jit(solution)/shard_map/dot_general | solution.py:30
  296.2 0.0 copy-start.2
  296.2 5.0 %multiply_reduce_fusion = (f32[]{:T(128)}, f32[1504,200]{0,1:T(8,128)S(1)}) fusion(bf16[6016,200]{0,1:T(8,128)(2,1)} %reshape.25, s32[]{:T(128)S(6)} %select_n.28, f32[752,1504]{1,0:T(8,128)S(1)} %get-tuple-element.9, s32[]{:T(128)S(6)} %select_n.27), kind=kOutput, calls=%fused_computation.8 | convolution fusion | flops 2715321600 | bytes 6648844 | tf_op jit(solution)/shard_map/dot_general | solution.py:41
  301.3 0.0 copy-done.2
  301.3 71.8 %all-reduce.6 = bf16[1504,200]{0,1:T(8,128)(2,1)S(1)} all-reduce(f32[1504,200]{0,1:T(8,128)S(1)} %get-tuple-element.7), channel_id=1, replica_groups=mesh['gx'=8,'gy'=4] {'gx'}, use_global_device_ids=true, to_apply=%region_2.3 | all-reduce | flops 300800 | bytes 1804800 | tf_op jit(solution)/shard_map/psum | solution.py:50
  373.1 0.0 copy-start.1
  373.1 7.1 %convolution_bitcast_fusion = f32[2500,200]{0,1:T(8,128)} fusion(bf16[1504,2500]{0,1:T(8,128)(2,1)} %param.4, bf16[1504,200]{0,1:T(8,128)(2,1)S(1)} %all-reduce.6), kind=kOutput, calls=%fused_computation.3 | convolution fusion | flops 1504000000 | bytes 10121600 | tf_op jit(solution)/shard_map/dot_general | solution.py:52
  380.2 0.0 copy-start.3
  380.2 24.7 %fusion = f32[2500,56]{0,1:T(8,128)S(1)} fusion(f32[2500,200]{0,1:T(8,128)} %convolution_bitcast_fusion), kind=kCustom, calls=%all-reduce-scatter | all-reduce-scatter fusion | flops 560001 | bytes 2560512
  404.9 1.9 collective-permute-start
  406.8 0.0 copy-done.3
  406.8 0.6 dynamic-slice.5
  408.1 41.9 %all-reduce.2 = (f32[]{:T(128)}, f32[]{:T(128)}) all-reduce(f32[]{:T(128)} %get-tuple-element.6, f32[]{:T(128)} %get-tuple-element.8), channel_id=1, replica_groups=mesh['gx'=8,'gy'=4] {'gx','gy'}, use_global_device_ids=true, to_apply=%region_5.6 | all-reduce | flops 2 | bytes 16 | tf_op jit(solution)/shard_map/psum | solution.py:49
  451.3 0.0 collective-permute-done
  451.3 0.4 concatenate
  451.7 0.9 constant_dynamic-slice_fusion
  452.6 0.0 copy-done.1
  (3 shorter events, 0.0 us)
Async XLA Ops:
  7.2 1.2 copy-start
  7.2 103.0 %all-gather.10.cloned.1.call-start = ((), (), s32[]{:S(2)}) async-start(), calls=%async_computation.1 | async-start | bytes 3072000 | tf_op jit(solution)/shard_map/all_gather | solution.py:16
  86.8 126.1 %all-gather.12.cloned.1.call-start = ((), (), s32[]{:S(2)}) async-start(), calls=%async_computation.2 | async-start | bytes 5529600 | tf_op jit(solution)/shard_map/all_gather | solution.py:24
  130.8 151.7 %all-gather.8.cloned.1.call-start = ((), (), s32[]{:S(2)}) async-start(), calls=%async_computation | async-start | bytes 12288000 | tf_op jit(solution)/shard_map/all_gather | solution.py:9
  296.2 5.0 %copy-start.2 = (f32[752,1504]{1,0:T(8,128)}, f32[752,1504]{1,0:T(8,128)S(1)}, u32[]{:S(2)}) copy-start(f32[752,1504]{1,0:T(8,128)S(1)} %get-tuple-element.9) | copy-start | bytes 13572100
  373.1 79.5 %copy-start.1 = (bf16[2500,200]{0,1:T(8,128)(2,1)S(1)}, bf16[2500,200]{0,1:T(8,128)(2,1)}, u32[]{:S(2)}) copy-start(bf16[2500,200]{0,1:T(8,128)(2,1)} %param.3) | copy-start | bytes 3000004
  380.2 26.7 %copy-start.3 = (u32[32]{0:T(128)S(1)}, u32[32]{0:T(128)}, u32[]{:S(2)}) copy-start(u32[32]{0:T(128)} %constant.45) | copy-start | bytes 388
  404.9 46.4 %collective-permute-start = (f32[2500,18]{0,1:T(8,128)S(1)}, f32[2500,18]{0,1:T(8,128)S(1)}, u32[]{:S(2)}, u32[]{:S(2)}) collective-permute-start(f32[2500,18]{0,1:T(8,128)S(1)} %slice), channel_id=1, source_target_pairs={{0,1},{1,2},{2,3},{4,5},{5,6},{6,7},{8,9},{9,10},{10,11},{12,13},{... | collective-permute-start | bytes 540008
Sparse Core Ops, SparseCore 0:
  86.9 23.1 all-gather.9
  130.9 82.0 all-gather.11
  217.9 64.4 all-gather.7
